TPU v7x, 32 devices: a whole 2x2x4 slice. The times are simulated.
32 devices in a mesh: gx: 8 (over y, x, core), gy: 4 (over z).
Axes of the slice: x: 2, y: 2, z: 4, core: 2. Of those that a mesh axis runs over, the one named last changes fastest.
Arguments:
- fields: float32 [5, 128, 128, 128], P(None, 'gx', 'gy'), may hold values from -6 to 6
- patch_weight: bfloat16 [2560, 512], replicated, may hold values from -0.125 to 0.125
- trainer_of: int32 [2048, 1], P(('gx', 'gy')), may hold values from 0 to 31; in each aligned block of 64 rows (0 to 63, 64 to 127, ...) at most 4 rows name the same one
- lag_index: int32 [16, 16, 16], P('gx', 'gy'), may hold values from 0 to 1
- w_in: bfloat16 [32, 512, 2048], P(('gx', 'gy')), may hold values from -0.25 to 0.25
- b_in: float32 [32, 2048], P(('gx', 'gy')), may hold values from -3 to 3
- w_out: bfloat16 [32, 2048, 512], P(('gx', 'gy')), may hold values from -0.125 to 0.125
- b_out: float32 [32, 512], P(('gx', 'gy')), may hold values from -3 to 3
Outputs:
- new_fields: float32 [5, 128, 128, 128], P(None, 'gx', 'gy')
- patch_gradient: float32 [2560, 512], replicated
- w_in_gradient: float32 [32, 512, 2048], P(('gx', 'gy'))
- b_in_gradient: float32 [32, 2048], P(('gx', 'gy'))
- w_out_gradient: float32 [32, 2048, 512], P(('gx', 'gy'))
- b_out_gradient: float32 [32, 512], P(('gx', 'gy'))
Inputs may be any that keep to these rules, and one draw needn't show every extreme that they name: `trainer_of`: among the 64 rows of one brick, no trainer is named more than 4 times.
All inputs are finite; a program needn't handle non-finite values.
Results may differ from a plain program's by a relative error of at most 0.0062.
Values may be sent and summed in bfloat16 or wider, within the bound.
A program may use at most 128 MiB of HBM per device.

v0:
```python
import jax
import jax.numpy as jnp
from jax import lax
from jax.sharding import PartitionSpec as P

FIELDS = 5
PATCH = 8
STEPS = 3
EMBED = 512
BLOCK_ROWS = 2


time_step = 0.2
viscosity = 0.5
drift_x = 0.6
drift_y = -0.4
drift_z = 0.3
error_weight = 0.0625


def with_halo(cells, sides, width):
    for axis, dim in sides:
        count = lax.axis_size(axis)
        ends = count - 1
        head = lax.slice_in_dim(cells, 0, width, axis=dim)
        tail = lax.slice_in_dim(cells, cells.shape[dim] - width, cells.shape[dim], axis=dim)
        cells = jnp.concatenate(
            [
                lax.ppermute(tail, axis, [(i, (i + 1) % count) for i in range(ends)]),
                cells,
                lax.ppermute(head, axis, [((i + 1) % count, i) for i in range(ends)]),
            ],
            axis=dim,
        )
    return cells


def shifted(padded, dimension, offset):
    window = [slice(None)]
    for other in (1, 2, 3):
        window.append(slice(2, padded.shape[other] - 2))
    window[dimension] = slice(2 + offset, padded.shape[dimension] - 2 + offset)
    return padded[tuple(window)]


def tendency(padded):
    gradients = []
    laplacian = 0.0
    for dimension in (1, 2, 3):
        back_two = shifted(padded, dimension, -2)
        back_one = shifted(padded, dimension, -1)
        middle = shifted(padded, dimension, 0)
        ahead_one = shifted(padded, dimension, 1)
        ahead_two = shifted(padded, dimension, 2)
        gradients.append((back_two - 8.0 * back_one + 8.0 * ahead_one - ahead_two) / 12.0)
        laplacian = (
            laplacian
            + (-back_two + 16.0 * back_one - 30.0 * middle + 16.0 * ahead_one - ahead_two) / 12.0
        )
    carried = drift_x * gradients[0] + drift_y * gradients[1] + drift_z * gradients[2]
    divergence = gradients[0][1] + gradients[1][2] + gradients[2][3]
    acoustic = jnp.stack(
        [divergence, gradients[0][4], gradients[1][4], gradients[2][4], divergence]
    )
    return viscosity * laplacian - carried - acoustic


def contract_rows(left, right):
    return lax.dot_general(
        left, right, (((0,), (0,)), ((), ())), preferred_element_type=jnp.float32
    )


def contract_cols(left, right):
    return lax.dot_general(
        left, right, (((1,), (1,)), ((), ())), preferred_element_type=jnp.float32
    )


def trainer_step(source, target, valid, w_first, b_first, w_second, b_second):
    pre = jnp.dot(source, w_first, preferred_element_type=jnp.float32) + b_first
    hidden = jax.nn.silu(pre).astype(jnp.bfloat16)
    predict = jnp.dot(hidden, w_second, preferred_element_type=jnp.float32) + b_second
    error = (error_weight * (predict - target.astype(jnp.float32)) * valid).astype(jnp.bfloat16)
    b_second_grad = jnp.sum(error.astype(jnp.float32), axis=0)
    w_second_grad = contract_rows(hidden, error)
    back = contract_cols(error, w_second)
    sigma = jax.nn.sigmoid(pre)
    pre_grad = (back * sigma * (1.0 + pre * (1.0 - sigma))).astype(jnp.bfloat16)
    b_first_grad = jnp.sum(pre_grad.astype(jnp.float32), axis=0)
    w_first_grad = contract_rows(source, pre_grad)
    source_grad = contract_cols(pre_grad, w_first).astype(jnp.bfloat16)
    return (source_grad, w_first_grad, b_first_grad, w_second_grad, b_second_grad)


def patchify(state):
    width_x, width_y, width_z = (state.shape[1], state.shape[2], state.shape[3])
    shaped = state.reshape(
        FIELDS, width_x // PATCH, PATCH, width_y // PATCH, PATCH, width_z // PATCH, PATCH
    )
    return shaped.transpose(1, 3, 5, 0, 2, 4, 6).reshape(-1, FIELDS * PATCH**3)


def pad_third(current):
    return jnp.pad(current, ((0, 0), (0, 0), (0, 0), (2, 2)))


def advance(fields):
    states = []
    current = fields
    for counter in range(STEPS):
        padded = with_halo(current, (("gx", 1), ("gy", 2)), 2)
        current = current + time_step * tendency(pad_third(padded))
        states.append(current)
    return states


def per_device(fields, patch_weight, trainer_of, lag_index, w_in, b_in, w_out, b_out):
    states = advance(fields)
    devices = lax.axis_size("gx") * lax.axis_size("gy")
    lag_rows = lag_index.reshape(-1, 1)
    picked = patchify(states[0].astype(jnp.bfloat16))
    picked = jnp.where(lag_rows == 1, patchify(states[1].astype(jnp.bfloat16)), picked)
    target = jnp.dot(
        patchify(states[-1].astype(jnp.bfloat16)), patch_weight, preferred_element_type=jnp.float32
    ).astype(jnp.bfloat16)
    patch_count = picked.shape[0]
    block_count = patch_count // BLOCK_ROWS
    slot_count = max(2, 2 * block_count // devices)
    owners = trainer_of[:, 0]
    onehot = (owners[:, None] == jnp.arange(devices, dtype=jnp.int32)[None, :]).astype(jnp.int32)
    within_rank = jnp.sum((jnp.cumsum(onehot, axis=0) - onehot) * onehot, axis=1)
    block_slot = owners * slot_count + within_rank

    def into_slots(rows):
        width = rows.shape[1]
        blocks = rows.reshape(block_count, BLOCK_ROWS, width)
        buffer = (
            jnp.zeros((devices * slot_count, BLOCK_ROWS, width), rows.dtype)
            .at[block_slot]
            .set(blocks)
        )
        return buffer.reshape(devices, slot_count, BLOCK_ROWS, width)

    valid_send = jnp.zeros((devices * slot_count,), jnp.bfloat16).at[block_slot].set(1.0)
    valid_send = valid_send.reshape(devices, slot_count)
    got_patches, got_target, got_valid = (
        lax.all_to_all(into_slots(picked), ("gx", "gy"), split_axis=0, concat_axis=0, tiled=True),
        lax.all_to_all(into_slots(target), ("gx", "gy"), split_axis=0, concat_axis=0, tiled=True),
        lax.all_to_all(valid_send, ("gx", "gy"), split_axis=0, concat_axis=0, tiled=True),
    )
    flat_patches = got_patches.reshape(-1, FIELDS * PATCH**3)
    source = jnp.dot(flat_patches, patch_weight, preferred_element_type=jnp.float32).astype(
        jnp.bfloat16
    )
    valid_rows = jnp.repeat(got_valid.astype(jnp.float32).reshape(-1), BLOCK_ROWS)[:, None]
    results = trainer_step(
        source, got_target.reshape(-1, EMBED), valid_rows, w_in[0], b_in[0], w_out[0], b_out[0]
    )
    partial_value = contract_rows(flat_patches, results[0])
    patch_gradient = lax.psum(partial_value, ("gx", "gy"))
    return (
        states[-1],
        patch_gradient,
        results[1][None],
        results[2][None],
        results[3][None],
        results[4][None],
    )


def solution(mesh):
    in_specs = (
        P(None, "gx", "gy", None),
        P(),
        P(("gx", "gy"), None),
        P("gx", "gy", None),
        P(("gx", "gy"), None, None),
        P(("gx", "gy"), None),
        P(("gx", "gy"), None, None),
        P(("gx", "gy"), None),
    )
    out_specs = (
        P(None, "gx", "gy", None),
        P(),
        P(("gx", "gy"), None, None),
        P(("gx", "gy"), None),
        P(("gx", "gy"), None, None),
        P(("gx", "gy"), None),
    )
    return jax.shard_map(
        per_device, mesh=mesh, in_specs=in_specs, out_specs=out_specs, check_vma=False
    )
```

profile of v0, /device:TPU:0, one launch (start us, length us, event | category | flops | bytes accessed | tf_op | source)
XLA Modules:
  0.0 457.8 jit_solution(11400775036131845433)
XLA Ops:
  7.2 1.2 fusion.64
  8.4 2.4 collective-permute-start
  10.8 1.3 collective-permute-start.1
  12.1 0.7 fusion.51
  12.9 0.8 select_reduce_fusion
  13.8 1.8 constant_dynamic-update-slice_fusion
  16.3 3.8 collective-permute-start.2
  20.1 1.3 collective-permute-start.3
  22.3 4.3 collective-permute-done.3
  26.6 1.6 select_maximum_fusion.8
  28.2 2.3 broadcast_multiply_fusion.2
  30.7 1.2 copy-done.6
  31.9 4.0 fusion.57
  35.9 1.1 copy-done.3
  37.0 4.0 collective-permute-start.4
  41.0 1.3 collective-permute-start.5
  42.4 1.0 scatter_custom_fusion.2
  43.4 0.7 all_to_all.16
  44.1 8.5 %all-to-all-start.2 = ((bf16[32,1,4]{2,1,0:T(2,128)(2,1)}), bf16[32,1,4]{2,1,0:T(2,128)(2,1)S(1)}, u32[]{:S(2)}, u32[]{:S(2)}) async-start(bf16[32,1,4]{2,1,0:T(2,128)(2,1)} %all_to_all.16), calls=%async_computation.2 | async-start | bytes 32768 | tf_op jit(solution)/shard_map/all_to_all | solution.py:150
  52.6 1.3 pad_maximum_fusion.13
  53.9 3.7 collective-permute-start.6
  57.5 1.8 collective-permute-start.7
  59.9 4.2 collective-permute-done.7
  64.1 3.5 select_maximum_fusion.4
  67.6 1.1 broadcast_multiply_fusion
  69.8 3.9 fusion.59
  73.7 1.1 copy-done.1
  74.8 1.3 collective-permute-start.8
  76.1 1.5 collective-permute-start.9
  78.3 14.4 %reshape.78 = bf16[5,2,8,4,8,16,8]{6,5,4,3,2,1,0:T(8,128)(2,1)} reshape(bf16[5,16,32,128]{3,2,1,0:T(8,128)(2,1)} %get-tuple-element.8) | data formatting | bytes 1310720 | tf_op jit(solution)/shard_map/reshape | solution.py:98
  92.7 10.7 %copy.18 = bf16[2,4,16,5,8,8,8]{6,5,4,3,2,1,0:T(8,128)(2,1)} copy(bf16[2,4,16,5,8,8,8]{6,2,5,1,4,0,3:T(8,128)(2,1)} %bitcast.69) | data formatting | bytes 1310720 | tf_op jit(solution)/shard_map/transpose | solution.py:101
  103.4 14.5 %reshape.79 = bf16[64,2,2560]{2,1,0:T(2,128)(2,1)} reshape(bf16[2,4,16,5,8,8,8]{6,5,4,3,2,1,0:T(8,128)(2,1)} %copy.18) | data formatting | bytes 1310720 | tf_op jit(solution)/shard_map/reshape | solution.py:101
  117.9 14.4 %reshape.76 = bf16[5,2,8,4,8,16,8]{6,5,4,3,2,1,0:T(8,128)(2,1)} reshape(bf16[5,16,32,128]{3,2,1,0:T(8,128)(2,1)} %get-tuple-element.10) | data formatting | bytes 1310720 | tf_op jit(solution)/shard_map/reshape | solution.py:98
  132.4 10.6 %copy.17 = bf16[2,4,16,5,8,8,8]{6,5,4,3,2,1,0:T(8,128)(2,1)} copy(bf16[2,4,16,5,8,8,8]{6,2,5,1,4,0,3:T(8,128)(2,1)} %bitcast.70) | data formatting | bytes 1310720 | tf_op jit(solution)/shard_map/transpose | solution.py:101
  143.0 14.5 %reshape.77 = bf16[64,2,2560]{2,1,0:T(2,128)(2,1)} reshape(bf16[2,4,16,5,8,8,8]{6,5,4,3,2,1,0:T(8,128)(2,1)} %copy.17) | data formatting | bytes 1310720 | tf_op jit(solution)/shard_map/reshape | solution.py:101
  157.5 1.3 pad_maximum_fusion.10
  158.7 3.4 collective-permute-start.10
  162.1 1.5 collective-permute-start.11
  164.4 4.3 collective-permute-done.11
  168.7 3.5 select_maximum_fusion
  172.2 1.1 broadcast_multiply_fusion.5
  174.4 4.1 fusion.55
  178.5 14.4 %reshape.82 = bf16[5,2,8,4,8,16,8]{6,5,4,3,2,1,0:T(8,128)(2,1)} reshape(bf16[5,16,32,128]{3,2,1,0:T(8,128)(2,1)} %get-tuple-element.6) | data formatting | bytes 1310720 | tf_op jit(solution)/shard_map/reshape | solution.py:98
  193.0 13.3 %copy.19 = bf16[2,4,16,5,8,8,8]{2,1,0,6,5,4,3:T(4,128)(2,1)} copy(bf16[2,4,16,5,8,8,8]{6,2,5,1,4,0,3:T(8,128)(2,1)} %bitcast.71) | data formatting | bytes 1310720 | tf_op jit(solution)/shard_map/transpose | solution.py:101
  206.3 7.3 %reshape.83 = bf16[128,2560]{0,1:T(8,128)(2,1)S(1)} reshape(bf16[2,4,16,5,8,8,8]{2,1,0,6,5,4,3:T(4,128)(2,1)} %copy.19) | data formatting | bytes 1310720 | tf_op jit(solution)/shard_map/reshape | solution.py:101
  214.2 0.8 broadcast_in_dim.41
  215.1 7.8 %scatter_fusion.1 = bf16[128,2,512]{2,1,0:T(2,128)(2,1)} fusion(bf16[128,2,512]{2,1,0:T(2,128)(2,1)} %broadcast_in_dim.41, s32[64]{0:T(128)S(1)} %fusion.52, bf16[64,2,512]{2,1,0:T(2,128)(2,1)S(1)} %reshape.99), kind=kCustom, calls=%fused_computation.1 | custom fusion | bytes 393472 | tf_op jit(solution)/shard_map/scatter | solution.py:141
  222.9 6.9 %all-to-all-start.1 = ((bf16[32,4,2,512]{3,2,1,0:T(2,128)(2,1)}), bf16[32,4,2,512]{3,2,1,0:T(2,128)(2,1)S(1)}, u32[]{:S(2)}, u32[]{:S(2)}) async-start(bf16[32,4,2,512]{3,2,1,0:T(2,128)(2,1)} %bitcast.11), calls=%async_computation.1 | async-start | bytes 524288 | tf_op jit(solution)/shard_map/all_to_all | solution.py:149
  229.9 2.1 broadcast_select_fusion
  232.0 1.7 broadcast_in_dim.39
  233.7 8.2 %scatter_fusion = bf16[128,2,2560]{2,1,0:T(2,128)(2,1)} fusion(bf16[128,2,2560]{2,1,0:T(2,128)(2,1)} %broadcast_in_dim.39, s32[64]{0:T(128)} %copy-done.13, bf16[64,2,2560]{2,1,0:T(2,128)(2,1)S(1)} %broadcast_select_fusion), kind=kCustom, calls=%fused_computation | custom fusion | bytes 1966336 | tf_op jit(solution)/shard_map/scatter | solution.py:141
  241.9 6.1 %all-to-all-start = ((bf16[32,4,2,2560]{3,2,1,0:T(2,128)(2,1)}), bf16[32,4,2,2560]{3,2,1,0:T(2,128)(2,1)}, u32[]{:S(2)}, u32[]{:S(2)}) async-start(bf16[32,4,2,2560]{3,2,1,0:T(2,128)(2,1)} %bitcast.72), calls=%async_computation | async-start | bytes 2621440 | tf_op jit(solution)/shard_map/all_to_all | solution.py:148
  248.4 0.9 reshape.86
  249.3 29.0 %all-to-all-done = bf16[32,4,2,2560]{3,2,1,0:T(2,128)(2,1)} async-done(((bf16[32,4,2,2560]{3,2,1,0:T(2,128)(2,1)}), bf16[32,4,2,2560]{3,2,1,0:T(2,128)(2,1)}, u32[]{:S(2)}, u32[]{:S(2)}) %all-to-all-start) | async-done | bytes 1310752 | tf_op jit(solution)/shard_map/all_to_all | solution.py:148
  278.4 4.1 reshape.81
  282.4 2.3 convolution_convert_fusion
  285.8 0.8 copy-done.14
  286.6 1.3 convert_reduce_fusion.1
  287.9 2.7 convert_reduce_fusion
  290.7 6.2 %fusion.46 = f32[2560,512]{1,0:T(8,128)} fusion(bf16[256,2560]{1,0:T(8,128)(2,1)} %reshape.81, bf16[256,2048]{1,0:T(8,128)(2,1)} %get-tuple-element.48, bf16[1,512,2048]{2,1,0:T(8,128)(2,1)} %param.12), kind=kOutput, calls=%fused_computation.96 | convolution fusion | flops 1208090624 | bytes 9699328 | tf_op jit(solution)/shard_map/dot_general | solution.py:69
  296.9 4.1 convolution_bitcast_fusion.1
  301.1 2.8 convolution_bitcast_fusion
  303.9 141.2 %all-reduce.5.cloned.1.call-done = f32[2560,512]{1,0:T(8,128)} async-done(((f32[2560,512]{1,0:T(8,128)}), f32[2560,512]{1,0:T(8,128)}) %all-reduce.5.cloned.1.call-update) | async-done | bytes 5242896 | tf_op jit(solution)/shard_map/psum | solution.py:161
  445.1 5.4 %copy.40 = f32[2560,512]{1,0:T(8,128)} copy(f32[2560,512]{1,0:T(8,128)} %all-reduce.5.cloned.1.call-done) | data formatting | bytes 10485760
  (80 shorter events, 8.1 us)
Async XLA Ops:
  7.2 206.5 %copy-start = (bf16[2560,512]{1,0:T(8,128)(2,1)S(1)}, bf16[2560,512]{1,0:T(8,128)(2,1)}, u32[]{:S(2)}) copy-start(bf16[2560,512]{1,0:T(8,128)(2,1)} %param.9) | copy-start | bytes 7864324
  8.4 5.4 %collective-permute-start = (f32[5,2,32,128]{3,2,1,0:T(8,128)S(1)}, f32[5,2,32,128]{3,2,1,0:T(8,128)S(1)}, u32[]{:S(2)}, u32[]{:S(2)}) collective-permute-start(f32[5,2,32,128]{3,2,1,0:T(8,128)S(1)} %get-tuple-element.42), channel_id=1, source_target_pairs={{0,4},{4,8},{8,12},{12,16},{16,20},{20,24},{24,28},{1,5},{5,9},{9,... | collective-permute-start | bytes 491528 | tf_op jit(solution)/shard_map/ppermute | solution.py:29
  10.8 5.4 %collective-permute-start.1 = (f32[5,2,32,128]{3,2,1,0:T(8,128)S(1)}, f32[5,2,32,128]{3,2,1,0:T(8,128)S(1)}, u32[]{:S(2)}, u32[]{:S(2)}) collective-permute-start(f32[5,2,32,128]{3,2,1,0:T(8,128)S(1)} %get-tuple-element.41), channel_id=1, source_target_pairs={{4,0},{8,4},{12,8},{16,12},{20,16},{24,20},{28,24},{5,1},{9,5},{13... | collective-permute-start | bytes 491528 | tf_op jit(solution)/shard_map/ppermute | solution.py:31
  16.3 6.0 %collective-permute-start.2 = (f32[5,20,2,128]{3,2,1,0:T(2,128)S(1)}, f32[5,20,2,128]{3,2,1,0:T(2,128)S(1)}, u32[]{:S(2)}, u32[]{:S(2)}) collective-permute-start(f32[5,20,2,128]{3,2,1,0:T(2,128)S(1)} %get-tuple-element.32), channel_id=1, source_target_pairs={{0,1},{1,2},{2,3},{4,5},{5,6},{6,7},{8,9},{9,10},{10,11},{12,13},{... | collective-permute-start | bytes 307208 | tf_op jit(solution)/shard_map/ppermute | solution.py:29
  20.1 6.6 %collective-permute-start.3 = (f32[5,20,2,128]{3,2,1,0:T(2,128)S(1)}, f32[5,20,2,128]{3,2,1,0:T(2,128)S(1)}, u32[]{:S(2)}, u32[]{:S(2)}) collective-permute-start(f32[5,20,2,128]{3,2,1,0:T(2,128)S(1)} %get-tuple-element.33), channel_id=1, source_target_pairs={{1,0},{2,1},{3,2},{5,4},{6,5},{7,6},{9,8},{10,9},{11,10},{13,12},{... | collective-permute-start | bytes 307208 | tf_op jit(solution)/shard_map/ppermute | solution.py:31
  30.6 1.3 copy-start.6
  31.9 10.4 %copy-start.12 = (s32[64,1]{0,1:T(1,128)S(1)}, s32[64,1]{0,1:T(1,128)}, u32[]{:S(2)}) copy-start(s32[64,1]{0,1:T(1,128)} %param.10) | copy-start | bytes 772
  35.9 1.1 copy-start.3
  37.0 15.6 %collective-permute-start.4 = (f32[5,2,32,128]{3,2,1,0:T(8,128)S(1)}, f32[5,2,32,128]{3,2,1,0:T(8,128)S(1)}, u32[]{:S(2)}, u32[]{:S(2)}) collective-permute-start(f32[5,2,32,128]{3,2,1,0:T(8,128)S(1)} %get-tuple-element.36), channel_id=1, source_target_pairs={{0,4},{4,8},{8,12},{12,16},{16,20},{20,24},{24,28},{1,5},{5,9},{9,... | collective-permute-start | bytes 491528 | tf_op jit(solution)/shard_map/ppermute | solution.py:29
  41.0 11.5 %collective-permute-start.5 = (f32[5,2,32,128]{3,2,1,0:T(8,128)S(1)}, f32[5,2,32,128]{3,2,1,0:T(8,128)S(1)}, u32[]{:S(2)}, u32[]{:S(2)}) collective-permute-start(f32[5,2,32,128]{3,2,1,0:T(8,128)S(1)} %get-tuple-element.37), channel_id=1, source_target_pairs={{4,0},{8,4},{12,8},{16,12},{20,16},{24,20},{28,24},{5,1},{9,5},{13... | collective-permute-start | bytes 491528 | tf_op jit(solution)/shard_map/ppermute | solution.py:31
  42.4 172.7 %copy-start.13 = (s32[64]{0:T(128)}, s32[64]{0:T(128)S(1)}, u32[]{:S(2)}) copy-start(s32[64]{0:T(128)S(1)} %fusion.52) | copy-start | bytes 772
  44.1 178.8 %all-to-all-start.2 = ((bf16[32,1,4]{2,1,0:T(2,128)(2,1)}), bf16[32,1,4]{2,1,0:T(2,128)(2,1)S(1)}, u32[]{:S(2)}, u32[]{:S(2)}) async-start(bf16[32,1,4]{2,1,0:T(2,128)(2,1)} %all_to_all.16), calls=%async_computation.2 | async-start | bytes 32768 | tf_op jit(solution)/shard_map/all_to_all | solution.py:150
  52.6 6.8 %copy-start.4 = (f32[5,16,32,128]{3,2,1,0:T(8,128)S(1)}, f32[5,16,32,128]{3,2,1,0:T(8,128)}, u32[]{:S(2)}) copy-start(f32[5,16,32,128]{3,2,1,0:T(8,128)} %copy-done.3) | copy-start | bytes 3932164
  53.9 6.1 %collective-permute-start.6 = (f32[5,20,2,128]{3,2,1,0:T(2,128)S(1)}, f32[5,20,2,128]{3,2,1,0:T(2,128)S(1)}, u32[]{:S(2)}, u32[]{:S(2)}) collective-permute-start(f32[5,20,2,128]{3,2,1,0:T(2,128)S(1)} %get-tuple-element.30), channel_id=1, source_target_pairs={{0,1},{1,2},{2,3},{4,5},{5,6},{6,7},{8,9},{9,10},{10,11},{12,13},{... | collective-permute-start | bytes 307208 | tf_op jit(solution)/shard_map/ppermute | solution.py:29
  57.5 6.6 %collective-permute-start.7 = (f32[5,20,2,128]{3,2,1,0:T(2,128)S(1)}, f32[5,20,2,128]{3,2,1,0:T(2,128)S(1)}, u32[]{:S(2)}, u32[]{:S(2)}) collective-permute-start(f32[5,20,2,128]{3,2,1,0:T(2,128)S(1)} %get-tuple-element.31), channel_id=1, source_target_pairs={{1,0},{2,1},{3,2},{5,4},{6,5},{7,6},{9,8},{10,9},{11,10},{13,12},{... | collective-permute-start | bytes 307208 | tf_op jit(solution)/shard_map/ppermute | solution.py:31
  69.8 7.7 %copy-start.11 = (s32[2,4,16]{2,1,0:T(4,128)S(1)}, s32[2,4,16]{2,1,0:T(4,128)}, u32[]{:S(2)}) copy-start(s32[2,4,16]{2,1,0:T(4,128)} %param.11) | copy-start | bytes 1540
  73.7 1.1 copy-start.1
  74.8 82.7 %collective-permute-start.8 = (f32[5,2,32,128]{3,2,1,0:T(8,128)S(1)}, f32[5,2,32,128]{3,2,1,0:T(8,128)S(1)}, u32[]{:S(2)}, u32[]{:S(2)}) collective-permute-start(f32[5,2,32,128]{3,2,1,0:T(8,128)S(1)} %get-tuple-element.34), channel_id=1, source_target_pairs={{0,4},{4,8},{8,12},{12,16},{16,20},{20,24},{24,28},{1,5},{5,9},{9,... | collective-permute-start | bytes 491528 | tf_op jit(solution)/shard_map/ppermute | solution.py:29
  76.1 81.4 %collective-permute-start.9 = (f32[5,2,32,128]{3,2,1,0:T(8,128)S(1)}, f32[5,2,32,128]{3,2,1,0:T(8,128)S(1)}, u32[]{:S(2)}, u32[]{:S(2)}) collective-permute-start(f32[5,2,32,128]{3,2,1,0:T(8,128)S(1)} %get-tuple-element.35), channel_id=1, source_target_pairs={{4,0},{8,4},{12,8},{16,12},{20,16},{24,20},{28,24},{5,1},{9,5},{13... | collective-permute-start | bytes 491528 | tf_op jit(solution)/shard_map/ppermute | solution.py:31
  157.5 6.2 %copy-start.2 = (f32[5,16,32,128]{3,2,1,0:T(8,128)S(1)}, f32[5,16,32,128]{3,2,1,0:T(8,128)}, u32[]{:S(2)}) copy-start(f32[5,16,32,128]{3,2,1,0:T(8,128)} %copy-done.1) | copy-start | bytes 3932164
  158.7 5.6 %collective-permute-start.10 = (f32[5,20,2,128]{3,2,1,0:T(2,128)S(1)}, f32[5,20,2,128]{3,2,1,0:T(2,128)S(1)}, u32[]{:S(2)}, u32[]{:S(2)}) collective-permute-start(f32[5,20,2,128]{3,2,1,0:T(2,128)S(1)} %get-tuple-element.26), channel_id=1, source_target_pairs={{0,1},{1,2},{2,3},{4,5},{5,6},{6,7},{8,9},{9,10},{10,11},{12,13},{... | collective-permute-start | bytes 307208 | tf_op jit(solution)/shard_map/ppermute | solution.py:29
  162.1 6.6 %collective-permute-start.11 = (f32[5,20,2,128]{3,2,1,0:T(2,128)S(1)}, f32[5,20,2,128]{3,2,1,0:T(2,128)S(1)}, u32[]{:S(2)}, u32[]{:S(2)}) collective-permute-start(f32[5,20,2,128]{3,2,1,0:T(2,128)S(1)} %get-tuple-element.27), channel_id=1, source_target_pairs={{1,0},{2,1},{3,2},{5,4},{6,5},{7,6},{9,8},{10,9},{11,10},{13,12},{... | collective-permute-start | bytes 307208 | tf_op jit(solution)/shard_map/ppermute | solution.py:31
  222.9 19.0 %all-to-all-start.1 = ((bf16[32,4,2,512]{3,2,1,0:T(2,128)(2,1)}), bf16[32,4,2,512]{3,2,1,0:T(2,128)(2,1)S(1)}, u32[]{:S(2)}, u32[]{:S(2)}) async-start(bf16[32,4,2,512]{3,2,1,0:T(2,128)(2,1)} %bitcast.11), calls=%async_computation.1 | async-start | bytes 524288 | tf_op jit(solution)/shard_map/all_to_all | solution.py:149
  241.9 36.4 %all-to-all-start = ((bf16[32,4,2,2560]{3,2,1,0:T(2,128)(2,1)}), bf16[32,4,2,2560]{3,2,1,0:T(2,128)(2,1)}, u32[]{:S(2)}, u32[]{:S(2)}) async-start(bf16[32,4,2,2560]{3,2,1,0:T(2,128)(2,1)} %bitcast.72), calls=%async_computation | async-start | bytes 2621440 | tf_op jit(solution)/shard_map/all_to_all | solution.py:148
  248.0 197.1 %all-reduce.5.cloned.1.call-start = ((), (), s32[]{:S(2)}) async-start(), calls=%async_computation.3 | async-start | bytes 10485760 | tf_op jit(solution)/shard_map/psum | solution.py:161
  282.4 2.3 copy-start.5
  282.4 2.3 copy-start.10
  284.7 1.0 copy-start.9
  284.8 1.8 copy-start.14
  284.8 1.8 copy-start.15
  285.5 2.4 copy-start.7
  296.9 4.1 copy-start.8
Sparse Core Ops, SparseCore 0:
  297.0 147.9 all-reduce.4
where the time goes:
time: 466 us; the launch traced here: 458 us
  waiting for transfers between devices  185 us (40%)
  local copies, waits for them, and re-layouts  154 us (33%)
  starting transfers between devices  48.8 us (10%)
  other arithmetic  34.4 us (7%)
  matrix products  20.8 us (4%)
  between operations  15.1 us (3%)
    psum x1, waiting for transfers between devices, per_device(): patch_gradient = lax.psum(partial_value, ('gx', 'gy'))  141 us
    reshape x3, local copies, waits for them, and re-layouts, patchify(): state.reshape(FIELDS, width_x // PATCH, PATCH, width_y // PATCH, PATCH, w...  43.3 us
    reshape x3, local copies, waits for them, and re-layouts, patchify(): shaped.transpose(1, 3, 5, 0, 2, 4, 6).reshape(-1, FIELDS * PATCH ** 3)  36.3 us
    transpose x3, local copies, waits for them, and re-layouts, patchify(): shaped.transpose(1, 3, 5, 0, 2, 4, 6).reshape(-1, FIELDS * PATCH ** 3)  34.6 us
    all_to_all x1, waiting for transfers between devices, per_device(): lax.all_to_all(into_slots(picked), ('gx', 'gy'), split_axis=0, concat_axi...  29 us
    ppermute x6, starting transfers between devices, with_halo(): lax.ppermute(tail, axis, [(i, (i + 1) % count) for i in range(ends)])  18.6 us
    scatter x2, local copies, waits for them, and re-layouts, into_slots(): buffer = jnp.zeros((devices * slot_count, BLOCK_ROWS, width), rows.dtype)...  16 us
    ppermute x6, waiting for transfers between devices, with_halo(): lax.ppermute(head, axis, [((i + 1) % count, i) for i in range(ends)])  13.3 us
  transfers between devices with their start and end apart: 16, of which 9 were waited for; matrix products, arithmetic and copies ran while one was open for 37% of the time, Pallas kernels for 0%

commit v1 on v0

--- a/solution.py
+++ b/solution.py
@@ -1,6 +1,8 @@
 import jax
 import jax.numpy as jnp
 from jax import lax
+from jax.experimental import pallas as pl
+from jax.experimental.pallas import tpu as pltpu
 from jax.sharding import PartitionSpec as P
 
 FIELDS = 5
@@ -93,12 +95,48 @@
     return (source_grad, w_first_grad, b_first_grad, w_second_grad, b_second_grad)
 
 
+def patch_kernel(cells_ref, rows_ref, *turned):
+    count, inner, lanes = rows_ref.shape[0], cells_ref.shape[1], turned[0].shape[1]
+    for part, piece in enumerate(turned):
+        cells = cells_ref[0, part * lanes : min(inner, (part + 1) * lanes), :]
+        if cells.shape[0] < lanes:
+            cells = jnp.concatenate(
+                [cells, jnp.zeros((lanes - cells.shape[0], cells.shape[1]), cells.dtype)], axis=0
+            )
+        piece[...] = cells.T
+    parts = []
+    for offset in range(PATCH):
+        for part, piece in enumerate(turned):
+            rows = piece[pl.ds(offset, count, stride=PATCH), :]
+            parts.append(rows[:, : min(lanes, inner - part * lanes)])
+    rows_ref[...] = jnp.concatenate(parts, axis=1).astype(rows_ref.dtype)
+
+
 def patchify(state):
     width_x, width_y, width_z = (state.shape[1], state.shape[2], state.shape[3])
-    shaped = state.reshape(
-        FIELDS, width_x // PATCH, PATCH, width_y // PATCH, PATCH, width_z // PATCH, PATCH
-    )
-    return shaped.transpose(1, 3, 5, 0, 2, 4, 6).reshape(-1, FIELDS * PATCH**3)
+    shaped = state.reshape(FIELDS, width_x // PATCH, PATCH, width_y // PATCH, PATCH, width_z)
+    cells = shaped.transpose(1, 3, 0, 2, 4, 5).reshape(-1, FIELDS * PATCH * PATCH, width_z)
+    columns, inner = cells.shape[0], cells.shape[1]
+    count = width_z // PATCH
+    return pl.pallas_call(
+        patch_kernel,
+        grid=(columns,),
+        out_shape=jax.ShapeDtypeStruct((columns * count, inner * PATCH), jnp.bfloat16),
+        in_specs=[pl.BlockSpec((1, inner, width_z), lambda i: (i, 0, 0))],
+        out_specs=pl.BlockSpec((count, inner * PATCH), lambda i: (i, 0)),
+        scratch_shapes=[pltpu.VMEM((width_z, 128), jnp.float32)] * pl.cdiv(inner, 128),
+        cost_estimate=pl.CostEstimate(
+            flops=8 * cells.size, bytes_accessed=6 * cells.size, transcendentals=0
+        ),
+    )(cells)
+
+
+def pick(first, second, lag_index):
+    count_x, count_y, count_z = lag_index.shape
+    lag = jnp.repeat(lag_index, PATCH, axis=2)
+    lag = lag.reshape(1, count_x, 1, count_y, 1, count_z * PATCH)
+    shape = (FIELDS, count_x, PATCH, count_y, PATCH, count_z * PATCH)
+    return jnp.where(lag == 1, second.reshape(shape), first.reshape(shape)).reshape(first.shape)
 
 
 def pad_third(current):
@@ -118,11 +156,11 @@
 def per_device(fields, patch_weight, trainer_of, lag_index, w_in, b_in, w_out, b_out):
     states = advance(fields)
     devices = lax.axis_size("gx") * lax.axis_size("gy")
-    lag_rows = lag_index.reshape(-1, 1)
-    picked = patchify(states[0].astype(jnp.bfloat16))
-    picked = jnp.where(lag_rows == 1, patchify(states[1].astype(jnp.bfloat16)), picked)
+    picked = patchify(pick(states[0], states[1], lag_index))
+    embed = patch_weight.shape[1]
+    weight = patch_weight.reshape(-1, PATCH, embed).transpose(1, 0, 2).reshape(-1, embed)
     target = jnp.dot(
-        patchify(states[-1].astype(jnp.bfloat16)), patch_weight, preferred_element_type=jnp.float32
+        patchify(states[-1]), weight, preferred_element_type=jnp.float32
     ).astype(jnp.bfloat16)
     patch_count = picked.shape[0]
     block_count = patch_count // BLOCK_ROWS
@@ -132,33 +170,33 @@
     within_rank = jnp.sum((jnp.cumsum(onehot, axis=0) - onehot) * onehot, axis=1)
     block_slot = owners * slot_count + within_rank
 
-    def into_slots(rows):
-        width = rows.shape[1]
-        blocks = rows.reshape(block_count, BLOCK_ROWS, width)
-        buffer = (
-            jnp.zeros((devices * slot_count, BLOCK_ROWS, width), rows.dtype)
-            .at[block_slot]
-            .set(blocks)
-        )
-        return buffer.reshape(devices, slot_count, BLOCK_ROWS, width)
-
-    valid_send = jnp.zeros((devices * slot_count,), jnp.bfloat16).at[block_slot].set(1.0)
-    valid_send = valid_send.reshape(devices, slot_count)
-    got_patches, got_target, got_valid = (
-        lax.all_to_all(into_slots(picked), ("gx", "gy"), split_axis=0, concat_axis=0, tiled=True),
-        lax.all_to_all(into_slots(target), ("gx", "gy"), split_axis=0, concat_axis=0, tiled=True),
-        lax.all_to_all(valid_send, ("gx", "gy"), split_axis=0, concat_axis=0, tiled=True),
-    )
-    flat_patches = got_patches.reshape(-1, FIELDS * PATCH**3)
-    source = jnp.dot(flat_patches, patch_weight, preferred_element_type=jnp.float32).astype(
+    patch_slot = jnp.repeat(block_slot, BLOCK_ROWS) * BLOCK_ROWS
+    patch_slot = patch_slot + jnp.arange(patch_count, dtype=jnp.int32) % BLOCK_ROWS
+    slot_rows = slot_count * BLOCK_ROWS
+    place = (
+        jnp.arange(devices * slot_rows, dtype=jnp.int32)[:, None] == patch_slot[None, :]
+    ).astype(jnp.bfloat16)
+
+    def exchange(rows):
+        packed = jnp.dot(place, rows, preferred_element_type=jnp.float32).astype(jnp.bfloat16)
+        packed = packed.reshape(devices, slot_rows, rows.shape[1])
+        got = lax.all_to_all(packed, ("gx", "gy"), split_axis=0, concat_axis=0, tiled=True)
+        return got.reshape(devices * slot_rows, rows.shape[1])
+
+    flat_patches = exchange(picked)
+    got_target = exchange(jnp.concatenate([target, jnp.ones((patch_count, 128), jnp.bfloat16)], 1))
+    source = jnp.dot(flat_patches, weight, preferred_element_type=jnp.float32).astype(
         jnp.bfloat16
     )
-    valid_rows = jnp.repeat(got_valid.astype(jnp.float32).reshape(-1), BLOCK_ROWS)[:, None]
+    valid_rows = got_target[:, embed : embed + 1].astype(jnp.float32)
     results = trainer_step(
-        source, got_target.reshape(-1, EMBED), valid_rows, w_in[0], b_in[0], w_out[0], b_out[0]
+        source, got_target[:, :embed], valid_rows, w_in[0], b_in[0], w_out[0], b_out[0]
     )
     partial_value = contract_rows(flat_patches, results[0])
-    patch_gradient = lax.psum(partial_value, ("gx", "gy"))
+    share = lax.psum_scatter(partial_value, ("gx", "gy"), scatter_dimension=0, tiled=True)
+    summed = lax.all_gather(share.astype(jnp.bfloat16), ("gx", "gy"), axis=0, tiled=True)
+    summed = summed.reshape(PATCH, -1, embed).transpose(1, 0, 2).reshape(-1, embed)
+    patch_gradient = summed.astype(jnp.float32)
     return (
         states[-1],
         patch_gradient,

time: 466 us -> 408 us (0.88); the launches traced: 458 us -> 407 us
  local copies, waits for them, and re-layouts: 154 us -> 17.6 us
  waiting for transfers between devices: 185 us -> 244 us
  Pallas kernels: 0 us -> 12.1 us
  other arithmetic: 34.4 us -> 40 us
  starting transfers between devices: 48.8 us -> 53.7 us
    reduce_scatter x0 -> x1, waiting for transfers between devices: none -> 155 us  [per_device(): lax.psum_scatter(partial_value, ('gx', 'gy'), scatter_dimension=0, tiled=...]
    psum x1 -> x0, waiting for transfers between devices: 141 us -> none  [per_device(): patch_gradient = lax.psum(partial_value, ('gx', 'gy'))]
    all_gather x0 -> x1, waiting for transfers between devices: none -> 53 us  [per_device(): lax.all_gather(share.astype(jnp.bfloat16), ('gx', 'gy'), axis=0, tiled=True)]
    reshape x3 -> x1, local copies, waits for them, and re-layouts: 43.3 us -> 1.35 us  [patchify(): state.reshape(FIELDS, width_x // PATCH, PATCH, width_y // PATCH, PATCH, w...]
    reshape x5 -> x0, local copies, waits for them, and re-layouts: 40.5 us -> none  [the longest x3 36.3 us: patchify(): shaped.transpose(1, 3, 5, 0, 2, 4, 6).reshape(-1, FIELDS * PATCH ** 3)]
    transpose x3 -> x1, local copies, waits for them, and re-layouts: 34.6 us -> 4.11 us  [per_device(): patch_weight.reshape(-1, PATCH, embed).transpose(1, 0, 2).reshape(-1, embed)]
    scatter x3 -> x0, local copies, waits for them, and re-layouts: 17 us -> none  [the longest x2 16 us: into_slots(): buffer = jnp.zeros((devices * slot_count, BLOCK_ROWS, width), rows.dtype)...]
    ppermute x6, waiting for transfers between devices: 13.3 us -> 1.09 us  [with_halo(): lax.ppermute(head, axis, [((i + 1) % count, i) for i in range(ends)])]
  transfers between devices with their start and end apart: 16 -> 16, of which waited for: 9 -> 10; matrix products, arithmetic and copies ran while one was open for 37% -> 5% of each run, Pallas kernels for 0% -> 1%
where the time goes in v1:
time: 408 us; the launch traced here: 407 us
  waiting for transfers between devices  244 us (60%)
  starting transfers between devices  53.7 us (13%)
  other arithmetic  40 us (10%)
  matrix products  25 us (6%)
  local copies, waits for them, and re-layouts  17.6 us (4%)
  between operations  14.7 us (4%)
  Pallas kernels  12.1 us (3%)
    reduce_scatter x1, waiting for transfers between devices, per_device(): lax.psum_scatter(partial_value, ('gx', 'gy'), scatter_dimension=0, tiled=...  155 us
    all_gather x1, waiting for transfers between devices, per_device(): lax.all_gather(share.astype(jnp.bfloat16), ('gx', 'gy'), axis=0, tiled=True)  53 us
    all_to_all x2, waiting for transfers between devices, exchange(): lax.all_to_all(packed, ('gx', 'gy'), split_axis=0, concat_axis=0, tiled=T...  29.1 us
    ppermute x6, starting transfers between devices, with_halo(): lax.ppermute(tail, axis, [(i, (i + 1) % count) for i in range(ends)])  26.1 us
    all_to_all x2, starting transfers between devices, exchange(): lax.all_to_all(packed, ('gx', 'gy'), split_axis=0, concat_axis=0, tiled=T...  19.5 us
    pallas_call x2, Pallas kernels, patchify(): pl.pallas_call(patch_kernel, grid=(columns,), out_shape=jax.ShapeDtypeStr...  12.1 us
    concatenate x5, other arithmetic, with_halo(): jnp.concatenate([lax.ppermute(tail, axis, [(i, (i + 1) % count) for i in...  11.4 us
    dot_general x3, matrix products, contract_rows(): lax.dot_general(left, right, (((0,), (0,)), ((), ())), preferred_element_...  10.7 us
  transfers between devices with their start and end apart: 16, of which 10 were waited for; matrix products, arithmetic and copies ran while one was open for 5% of the time, Pallas kernels for 1%

profile of v1, /device:TPU:0, one launch (start us, length us, event | category | flops | bytes accessed | tf_op | source)
XLA Modules:
  0.0 406.8 jit_solution(12653624537642688695)
XLA Ops:
  7.2 1.2 fusion.68
  8.4 2.4 collective-permute-start
  10.8 1.3 collective-permute-start.1
  12.1 0.7 fusion.62
  12.9 0.8 select_reduce_fusion
  13.8 1.8 constant_dynamic-update-slice_fusion
  15.6 0.5 collective-permute-done.1
  16.3 1.3 collective-permute-start.3
  17.6 4.6 %collective-permute-start.2 = (f32[5,20,2,128]{3,2,1,0:T(2,128)S(1)}, f32[5,20,2,128]{3,2,1,0:T(2,128)S(1)}, u32[]{:S(2)}, u32[]{:S(2)}) collective-permute-start(f32[5,20,2,128]{3,2,1,0:T(2,128)S(1)} %get-tuple-element.26), channel_id=1, source_target_pairs={{0,1},{1,2},{2,3},{4,5},{5,6},{6,7},{8,9},{9,10},{10,11},{12,13},{... | collective-permute-start | bytes 307208 | tf_op jit(solution)/shard_map/ppermute | solution.py:31
  22.5 0.3 collective-permute-done.3
  22.8 1.5 collective-permute-done.2
  24.4 1.6 select_maximum_fusion.8
  25.9 2.3 broadcast_multiply_fusion.2
  28.5 1.2 copy-done.2
  29.6 3.3 fusion.28
  32.9 0.8 fusion.67
  33.7 1.3 collective-permute-start.5
  34.9 5.9 %collective-permute-start.4 = (f32[5,2,32,128]{3,2,1,0:T(8,128)}, f32[5,2,32,128]{3,2,1,0:T(8,128)}, u32[]{:S(2)}, u32[]{:S(2)}) collective-permute-start(f32[5,2,32,128]{3,2,1,0:T(8,128)} %get-tuple-element.30), channel_id=1, source_target_pairs={{0,4},{4,8},{8,12},{12,16},{16,20},{20,24},{24,28},{1,5},{5,9},{9,... | collective-permute-start | bytes 491528 | tf_op jit(solution)/shard_map/ppermute | solution.py:31
  41.1 4.1 %copy.24 = bf16[8,320,512]{2,1,0:T(8,128)(2,1)} copy(bf16[8,320,512]{2,0,1:T(8,128)(2,1)} %bitcast.88) | data formatting | bytes 5242880 | tf_op jit(solution)/shard_map/transpose | solution.py:161
  45.2 0.9 pad_maximum_fusion.13
  46.1 1.3 collective-permute-start.7
  47.4 4.8 %collective-permute-start.6 = (f32[5,20,2,128]{3,2,1,0:T(2,128)S(1)}, f32[5,20,2,128]{3,2,1,0:T(2,128)S(1)}, u32[]{:S(2)}, u32[]{:S(2)}) collective-permute-start(f32[5,20,2,128]{3,2,1,0:T(2,128)S(1)} %get-tuple-element.24), channel_id=1, source_target_pairs={{0,1},{1,2},{2,3},{4,5},{5,6},{6,7},{8,9},{9,10},{10,11},{12,13},{... | collective-permute-start | bytes 307208 | tf_op jit(solution)/shard_map/ppermute | solution.py:31
  52.3 1.3 fusion.56
  53.6 0.9 collective-permute-done.6
  54.5 4.4 %select_maximum_fusion.4 = f32[5,20,36,132]{3,2,1,0:T(8,128)S(1)} fusion(f32[5,20,2,128]{3,2,1,0:T(2,128)S(1)} %collective-permute-done.7, f32[5,20,2,128]{3,2,1,0:T(2,128)S(1)} %collective-permute-done.6, f32[5,2,32,128]{3,2,1,0:T(8,128)} %collective-permute-done.5, f32[5,16,32,128]{3,2,1,0:T(8,128)S(1)} %fusion.28, f32[5,2,32,128]{3,2,1,0:T(8,128)} %collective-permute-done.4), kind=kLoop, calls=%fused_computation.8 | loop fusion | flops 5702400 | bytes 3744000 | tf_op jit(solution)/shard_map/concatenate | solution.py:29
  58.9 1.1 broadcast_multiply_fusion
  60.0 1.6 maximum_maximum_fusion
  61.6 0.5 broadcast_multiply_fusion.1
  62.3 4.2 %fusion.25 = f32[5,16,32,128]{3,2,1,0:T(8,128)S(1)} fusion(f32[5,16,32,128]{3,2,1,0:T(8,128)S(1)} %fusion.28, f32[5,16,32,128]{3,2,1,0:T(8,128)S(1)} %constant_dynamic-update-slice_fusion.9, f32[5,16,32,128]{3,2,1,0:T(8,128)S(1)} %get-tuple-element.13, f32[5,16,32,128]{3,2,1,0:T(8,128)S(1)} %get-tuple-element.11, ...), kind=kLoop, calls=%fused_computation.72 | loop fusion | flops 14090240 | bytes 17367040 | tf_op jit(solution)/shard_map/add | solution.py:151
  66.6 1.3 collective-permute-start.9
  67.9 3.5 collective-permute-start.8
  71.4 1.0 collective-permute-done.8
  72.5 1.3 collective-permute-start.11
  73.8 4.9 %collective-permute-start.10 = (f32[5,20,2,128]{3,2,1,0:T(2,128)S(1)}, f32[5,20,2,128]{3,2,1,0:T(2,128)S(1)}, u32[]{:S(2)}, u32[]{:S(2)}) collective-permute-start(f32[5,20,2,128]{3,2,1,0:T(2,128)S(1)} %get-tuple-element.20), channel_id=1, source_target_pairs={{0,1},{1,2},{2,3},{4,5},{5,6},{6,7},{8,9},{9,10},{10,11},{12,13},{... | collective-permute-start | bytes 307208 | tf_op jit(solution)/shard_map/ppermute | solution.py:31
  79.2 1.5 collective-permute-done.10
  80.7 3.5 select_maximum_fusion
  84.3 1.1 broadcast_multiply_fusion.5
  85.3 0.4 maximum_maximum_fusion.1
  85.7 0.5 broadcast_multiply_fusion.4
  86.5 3.1 fusion.22
  89.6 1.3 copy.25
  91.1 6.0 %shard_map.128 = bf16[128,2560]{1,0:T(8,128)(2,1)} custom-call(f32[8,320,128]{2,1,0:T(8,128)} %bitcast.87), custom_call_target="tpu_custom_call" | custom-call | flops 2621440 | bytes 1966080 | tf_op jit(solution)/shard_map/pallas_call | solution.py:121
  97.1 2.5 convolution_convert_fusion.2
  99.6 0.9 fusion.53
  100.6 13.7 %all-to-all-start.1 = ((bf16[32,8,640]{2,1,0:T(8,128)(2,1)}), bf16[32,8,640]{2,1,0:T(8,128)(2,1)}, u32[]{:S(2)}, u32[]{:S(2)}) async-start(bf16[32,8,640]{2,1,0:T(8,128)(2,1)} %fusion.53), calls=%async_computation.1 | async-start | bytes 655360 | tf_op jit(solution)/shard_map/all_to_all | solution.py:183
  114.5 2.6 copy_select_fusion
  117.1 6.0 %shard_map.127 = bf16[128,2560]{1,0:T(8,128)(2,1)} custom-call(f32[8,320,128]{2,1,0:T(8,128)} %bitcast.86), custom_call_target="tpu_custom_call" | custom-call | flops 2621440 | bytes 1966080 | tf_op jit(solution)/shard_map/pallas_call | solution.py:121
  123.1 2.6 fusion.1
  125.8 5.8 %all-to-all-start = ((bf16[32,8,2560]{2,1,0:T(8,128)(2,1)}), bf16[32,8,2560]{2,1,0:T(8,128)(2,1)S(1)}, u32[]{:S(2)}, u32[]{:S(2)}) async-start(bf16[32,8,2560]{2,1,0:T(8,128)(2,1)} %fusion.1), calls=%async_computation | async-start | bytes 2621440 | tf_op jit(solution)/shard_map/all_to_all | solution.py:183
  131.9 1.0 multiply_reduce_fusion
  132.8 29.1 %all-to-all-done = bf16[32,8,2560]{2,1,0:T(8,128)(2,1)S(1)} async-done(((bf16[32,8,2560]{2,1,0:T(8,128)(2,1)}), bf16[32,8,2560]{2,1,0:T(8,128)(2,1)S(1)}, u32[]{:S(2)}, u32[]{:S(2)}) %all-to-all-start) | async-done | bytes 1310752 | tf_op jit(solution)/shard_map/all_to_all | solution.py:183
  161.9 2.6 fusion.44
  164.5 0.7 convolution_add_fusion
  165.3 0.9 copy-done.12
  166.2 2.3 convert_reduce_fusion.1
  168.5 2.7 convert_reduce_fusion
  171.2 5.2 %fusion.16 = f32[2560,512]{1,0:T(8,128)} fusion(bf16[32,8,2560]{2,1,0:T(8,128)(2,1)S(1)} %all-to-all-done, bf16[256,2048]{1,0:T(8,128)(2,1)} %get-tuple-element.42, bf16[1,512,2048]{2,1,0:T(8,128)(2,1)S(1)} %copy-done), kind=kOutput, calls=%fused_computation.60 | convolution fusion | flops 1208090624 | bytes 9699328 | tf_op jit(solution)/shard_map/dot_general | solution.py:71
  176.4 155.4 %reduce-scatter.2.cloned.1.call-done = f32[80,512]{1,0:T(8,128)} async-done(((f32[2560,512]{1,0:T(8,128)}), f32[80,512]{1,0:T(8,128)}) %reduce-scatter.2.cloned.1.call-update) | async-done | bytes 163856 | tf_op jit(solution)/shard_map/reduce_scatter | solution.py:196
  331.8 1.6 convert_element_type.70
  333.4 2.7 convolution_bitcast_fusion.1
  336.2 2.8 convolution_bitcast_fusion
  339.0 53.0 %all-gather.2.cloned.1.call-done = bf16[2560,512]{1,0:T(8,128)(2,1)} async-done(((bf16[80,512]{1,0:T(8,128)(2,1)}), bf16[2560,512]{1,0:T(8,128)(2,1)}) %all-gather.2.cloned.1.call-update) | async-done | bytes 2621456 | tf_op jit(solution)/shard_map/all_gather | solution.py:197
  392.0 2.5 convert_bitcast_fusion
  394.5 5.4 %copy.30 = f32[320,8,512]{2,1,0:T(8,128)} copy(f32[320,8,512]{2,0,1:T(8,128)S(1)} %convert_bitcast_fusion) | data formatting | bytes 10485760 | tf_op jit(solution)/shard_map/convert_element_type | solution.py:199
  (71 shorter events, 2.7 us)
Async XLA Ops:
  7.2 157.3 %copy-start = (bf16[1,512,2048]{2,1,0:T(8,128)(2,1)S(1)}, bf16[1,512,2048]{2,1,0:T(8,128)(2,1)}, u32[]{:S(2)}) copy-start(bf16[1,512,2048]{2,1,0:T(8,128)(2,1)} %param.12) | copy-start | bytes 6291460
  8.4 5.4 %collective-permute-start = (f32[5,2,32,128]{3,2,1,0:T(8,128)S(1)}, f32[5,2,32,128]{3,2,1,0:T(8,128)S(1)}, u32[]{:S(2)}, u32[]{:S(2)}) collective-permute-start(f32[5,2,32,128]{3,2,1,0:T(8,128)S(1)} %get-tuple-element.36), channel_id=1, source_target_pairs={{0,4},{4,8},{8,12},{12,16},{16,20},{20,24},{24,28},{1,5},{5,9},{9,... | collective-permute-start | bytes 491528 | tf_op jit(solution)/shard_map/ppermute | solution.py:31
  10.8 5.4 %collective-permute-start.1 = (f32[5,2,32,128]{3,2,1,0:T(8,128)S(1)}, f32[5,2,32,128]{3,2,1,0:T(8,128)S(1)}, u32[]{:S(2)}, u32[]{:S(2)}) collective-permute-start(f32[5,2,32,128]{3,2,1,0:T(8,128)S(1)} %get-tuple-element.35), channel_id=1, source_target_pairs={{4,0},{8,4},{12,8},{16,12},{20,16},{24,20},{28,24},{5,1},{9,5},{13... | collective-permute-start | bytes 491528 | tf_op jit(solution)/shard_map/ppermute | solution.py:33
  16.3 6.6 %collective-permute-start.3 = (f32[5,20,2,128]{3,2,1,0:T(2,128)S(1)}, f32[5,20,2,128]{3,2,1,0:T(2,128)S(1)}, u32[]{:S(2)}, u32[]{:S(2)}) collective-permute-start(f32[5,20,2,128]{3,2,1,0:T(2,128)S(1)} %get-tuple-element.27), channel_id=1, source_target_pairs={{1,0},{2,1},{3,2},{5,4},{6,5},{7,6},{9,8},{10,9},{11,10},{13,12},{... | collective-permute-start | bytes 307208 | tf_op jit(solution)/shard_map/ppermute | solution.py:33
  17.6 6.8 %collective-permute-start.2 = (f32[5,20,2,128]{3,2,1,0:T(2,128)S(1)}, f32[5,20,2,128]{3,2,1,0:T(2,128)S(1)}, u32[]{:S(2)}, u32[]{:S(2)}) collective-permute-start(f32[5,20,2,128]{3,2,1,0:T(2,128)S(1)} %get-tuple-element.26), channel_id=1, source_target_pairs={{0,1},{1,2},{2,3},{4,5},{5,6},{6,7},{8,9},{9,10},{10,11},{12,13},{... | collective-permute-start | bytes 307208 | tf_op jit(solution)/shard_map/ppermute | solution.py:31
  28.3 1.3 copy-start.2
  29.6 11.2 %copy-start.11 = (s32[64,1]{0,1:T(1,128)S(1)}, s32[64,1]{0,1:T(1,128)}, u32[]{:S(2)}) copy-start(s32[64,1]{0,1:T(1,128)} %param.10) | copy-start | bytes 772
  33.7 11.6 %collective-permute-start.5 = (f32[5,2,32,128]{3,2,1,0:T(8,128)}, f32[5,2,32,128]{3,2,1,0:T(8,128)}, u32[]{:S(2)}, u32[]{:S(2)}) collective-permute-start(f32[5,2,32,128]{3,2,1,0:T(8,128)} %get-tuple-element.31), channel_id=1, source_target_pairs={{4,0},{8,4},{12,8},{16,12},{20,16},{24,20},{28,24},{5,1},{9,5},{13... | collective-permute-start | bytes 491528 | tf_op jit(solution)/shard_map/ppermute | solution.py:33
  34.9 10.3 %collective-permute-start.4 = (f32[5,2,32,128]{3,2,1,0:T(8,128)}, f32[5,2,32,128]{3,2,1,0:T(8,128)}, u32[]{:S(2)}, u32[]{:S(2)}) collective-permute-start(f32[5,2,32,128]{3,2,1,0:T(8,128)} %get-tuple-element.30), channel_id=1, source_target_pairs={{0,4},{4,8},{8,12},{12,16},{16,20},{20,24},{24,28},{1,5},{5,9},{9,... | collective-permute-start | bytes 491528 | tf_op jit(solution)/shard_map/ppermute | solution.py:31
  46.1 7.5 %collective-permute-start.7 = (f32[5,20,2,128]{3,2,1,0:T(2,128)S(1)}, f32[5,20,2,128]{3,2,1,0:T(2,128)S(1)}, u32[]{:S(2)}, u32[]{:S(2)}) collective-permute-start(f32[5,20,2,128]{3,2,1,0:T(2,128)S(1)} %get-tuple-element.25), channel_id=1, source_target_pairs={{1,0},{2,1},{3,2},{5,4},{6,5},{7,6},{9,8},{10,9},{11,10},{13,12},{... | collective-permute-start | bytes 307208 | tf_op jit(solution)/shard_map/ppermute | solution.py:33
  47.4 7.1 %collective-permute-start.6 = (f32[5,20,2,128]{3,2,1,0:T(2,128)S(1)}, f32[5,20,2,128]{3,2,1,0:T(2,128)S(1)}, u32[]{:S(2)}, u32[]{:S(2)}) collective-permute-start(f32[5,20,2,128]{3,2,1,0:T(2,128)S(1)} %get-tuple-element.24), channel_id=1, source_target_pairs={{0,1},{1,2},{2,3},{4,5},{5,6},{6,7},{8,9},{9,10},{10,11},{12,13},{... | collective-permute-start | bytes 307208 | tf_op jit(solution)/shard_map/ppermute | solution.py:31
  66.6 19.9 %copy-start.1 = (f32[5,16,32,128]{3,2,1,0:T(8,128)}, f32[5,16,32,128]{3,2,1,0:T(8,128)S(1)}, u32[]{:S(2)}) copy-start(f32[5,16,32,128]{3,2,1,0:T(8,128)S(1)} %fusion.25) | copy-start | bytes 3932164
  66.6 4.8 %collective-permute-start.9 = (f32[5,2,32,128]{3,2,1,0:T(8,128)S(1)}, f32[5,2,32,128]{3,2,1,0:T(8,128)S(1)}, u32[]{:S(2)}, u32[]{:S(2)}) collective-permute-start(f32[5,2,32,128]{3,2,1,0:T(8,128)S(1)} %get-tuple-element.29), channel_id=1, source_target_pairs={{4,0},{8,4},{12,8},{16,12},{20,16},{24,20},{28,24},{5,1},{9,5},{13... | collective-permute-start | bytes 491528 | tf_op jit(solution)/shard_map/ppermute | solution.py:33
  67.9 4.5 %collective-permute-start.8 = (f32[5,2,32,128]{3,2,1,0:T(8,128)S(1)}, f32[5,2,32,128]{3,2,1,0:T(8,128)S(1)}, u32[]{:S(2)}, u32[]{:S(2)}) collective-permute-start(f32[5,2,32,128]{3,2,1,0:T(8,128)S(1)} %get-tuple-element.28), channel_id=1, source_target_pairs={{0,4},{4,8},{8,12},{12,16},{16,20},{20,24},{24,28},{1,5},{5,9},{9,... | collective-permute-start | bytes 491528 | tf_op jit(solution)/shard_map/ppermute | solution.py:31
  72.5 6.7 %collective-permute-start.11 = (f32[5,20,2,128]{3,2,1,0:T(2,128)S(1)}, f32[5,20,2,128]{3,2,1,0:T(2,128)S(1)}, u32[]{:S(2)}, u32[]{:S(2)}) collective-permute-start(f32[5,20,2,128]{3,2,1,0:T(2,128)S(1)} %get-tuple-element.21), channel_id=1, source_target_pairs={{1,0},{2,1},{3,2},{5,4},{6,5},{7,6},{9,8},{10,9},{11,10},{13,12},{... | collective-permute-start | bytes 307208 | tf_op jit(solution)/shard_map/ppermute | solution.py:33
  73.8 7.0 %collective-permute-start.10 = (f32[5,20,2,128]{3,2,1,0:T(2,128)S(1)}, f32[5,20,2,128]{3,2,1,0:T(2,128)S(1)}, u32[]{:S(2)}, u32[]{:S(2)}) collective-permute-start(f32[5,20,2,128]{3,2,1,0:T(2,128)S(1)} %get-tuple-element.20), channel_id=1, source_target_pairs={{0,1},{1,2},{2,3},{4,5},{5,6},{6,7},{8,9},{9,10},{10,11},{12,13},{... | collective-permute-start | bytes 307208 | tf_op jit(solution)/shard_map/ppermute | solution.py:31
  89.6 1.5 copy-start.3
  97.1 17.2 %copy-start.10 = (s32[2,4,16]{2,1,0:T(4,128)S(1)}, s32[2,4,16]{2,1,0:T(4,128)}, u32[]{:S(2)}) copy-start(s32[2,4,16]{2,1,0:T(4,128)} %param.11) | copy-start | bytes 1540
  100.6 25.2 %all-to-all-start.1 = ((bf16[32,8,640]{2,1,0:T(8,128)(2,1)}), bf16[32,8,640]{2,1,0:T(8,128)(2,1)}, u32[]{:S(2)}, u32[]{:S(2)}) async-start(bf16[32,8,640]{2,1,0:T(8,128)(2,1)} %fusion.53), calls=%async_computation.1 | async-start | bytes 655360 | tf_op jit(solution)/shard_map/all_to_all | solution.py:183
  125.8 36.1 %all-to-all-start = ((bf16[32,8,2560]{2,1,0:T(8,128)(2,1)}), bf16[32,8,2560]{2,1,0:T(8,128)(2,1)S(1)}, u32[]{:S(2)}, u32[]{:S(2)}) async-start(bf16[32,8,2560]{2,1,0:T(8,128)(2,1)} %fusion.1), calls=%async_computation | async-start | bytes 2621440 | tf_op jit(solution)/shard_map/all_to_all | solution.py:183
  131.5 200.2 %reduce-scatter.2.cloned.1.call-start = ((), (), s32[]{:S(2)}) async-start(), calls=%async_computation.3 | async-start | bytes 5406720 | tf_op jit(solution)/shard_map/reduce_scatter | solution.py:196
  132.8 31.7 %copy-start.9 = (f32[1,2048]{1,0:T(1,128)S(1)}, f32[1,2048]{1,0:T(1,128)}, u32[]{:S(2)}) copy-start(f32[1,2048]{1,0:T(1,128)} %param.13) | copy-start | bytes 24580
  164.5 0.8 copy-start.7
  164.5 1.7 copy-start.12
  164.5 1.7 copy-start.13
  165.3 3.2 copy-start.5
  168.5 2.7 copy-start.14
  176.3 157.0 %copy-start.4 = (bf16[256,2048]{1,0:T(8,128)(2,1)S(1)}, bf16[256,2048]{1,0:T(8,128)(2,1)}, u32[]{:S(2)}) copy-start(bf16[256,2048]{1,0:T(8,128)(2,1)} %get-tuple-element.42) | copy-start | bytes 3145732
  176.3 157.0 %copy-start.8 = (bf16[256,512]{1,0:T(8,128)(2,1)S(1)}, bf16[256,512]{1,0:T(8,128)(2,1)}, u32[]{:S(2)}) copy-start(bf16[256,512]{1,0:T(8,128)(2,1)} %copy-done.7) | copy-start | bytes 786436
  176.4 215.7 %all-gather.2.cloned.1.call-start = ((), (), s32[]{:S(2)}) async-start(), calls=%async_computation.4 | async-start | bytes 2703360 | tf_op jit(solution)/shard_map/all_gather | solution.py:197
  333.4 2.8 copy-start.6
  333.4 2.8 copy-start.15
Sparse Core Ops, SparseCore 0:
  176.5 155.2 reduce-scatter.1
  335.2 56.8 all-gather.1
